TPU v7x, 32 devices: a whole 2x2x4 slice. The times are simulated.
32 devices in a mesh: dp: 8 (over y, x, core), tensor: 4 (over z).
Axes of the slice: x: 2, y: 2, z: 4, core: 2. Of those that a mesh axis runs over, the one named last changes fastest.
Arguments:
- hidden_in: bfloat16 [16384, 1024], P(('dp', 'tensor')), may hold values from -6 to 6
- cotangent: bfloat16 [16384, 1024], P(('dp', 'tensor')), may hold values from -6 to 6
- w_query: float32 [1024, 1024], P('dp', 'tensor'), may hold values from -0.1875 to 0.1875
- w_key: float32 [1024, 1024], P('dp', 'tensor'), may hold values from -0.1875 to 0.1875
- w_value: float32 [1024, 1024], P('dp', 'tensor'), may hold values from -0.1875 to 0.1875
- w_out: float32 [1024, 1024], P('dp', 'tensor'), may hold values from -2 to 2
- w_up: float32 [1024, 4096], P('dp', 'tensor'), may hold values from -0.1875 to 0.1875
- w_down: float32 [1024, 4096], P('dp', 'tensor'), may hold values from -0.09375 to 0.09375
- bias_query: float32 [1024], replicated, may hold values from -3 to 3
- bias_value: float32 [1024], replicated, may hold values from -3 to 3
- bias_out: float32 [1024], replicated, may hold values from -3 to 3
- bias_up: float32 [4096], replicated, may hold values from -3 to 3
- bias_down: float32 [1024], replicated, may hold values from -3 to 3
- gain_attn: float32 [1024], replicated, may hold values from 0.5 to 1.5
- shift_attn: float32 [1024], replicated, may hold values from -3 to 3
- gain_ffn: float32 [1024], replicated, may hold values from 0.5 to 1.5
- shift_ffn: float32 [1024], replicated, may hold values from -3 to 3
- valid_lengths: int32 [32], P('dp'), may hold values from 64 to 512, as said below
Outputs:
- output: bfloat16 [16384, 1024], P(('dp', 'tensor'))
- grad_hidden_in: bfloat16 [16384, 1024], P(('dp', 'tensor'))
- grad_w_query: float32 [1024, 1024], P('dp', 'tensor')
- grad_w_key: float32 [1024, 1024], P('dp', 'tensor')
- grad_w_value: float32 [1024, 1024], P('dp', 'tensor')
- grad_w_out: float32 [1024, 1024], P('dp', 'tensor')
- grad_w_up: float32 [1024, 4096], P('dp', 'tensor')
- grad_w_down: float32 [1024, 4096], P('dp', 'tensor')
- grad_bias_query: float32 [1024], replicated
- grad_bias_value: float32 [1024], replicated
- grad_bias_out: float32 [1024], replicated
- grad_bias_up: float32 [4096], replicated
- grad_bias_down: float32 [1024], replicated
- grad_gain_attn: float32 [1024], replicated
- grad_shift_attn: float32 [1024], replicated
- grad_gain_ffn: float32 [1024], replicated
- grad_shift_ffn: float32 [1024], replicated
Inputs may be any that keep to these rules, and one draw needn't show every extreme that they name: Each sequence's real tokens are its first valid_lengths positions; some sequence has all 512.
All inputs are finite; a program needn't handle non-finite values.
Results may differ from a plain program's by a relative error of at most 0.02.
Values may be sent and summed in bfloat16 or wider, within the bound.
A program may use at most 128 MiB of HBM per device.

v0:
```python
import math

import jax
import jax.numpy as jnp
from jax import lax
from jax.experimental import pallas as pl
from jax.experimental.pallas import tpu as pltpu
from jax.sharding import PartitionSpec as P

HEADS = 16
EPSILON = 1e-12
MASKED = -1e30
BF16 = jnp.bfloat16
F32 = jnp.float32

ORDER = (0, 2, 4, 6, 1, 3, 5, 7)
BIT_CORE, BIT_X, BIT_Y = 1, 2, 4


def matmul(left_side, right_side):
    return jnp.dot(left_side, right_side, preferred_element_type=F32)


def contract_rows(left_side, right_side):
    return lax.dot_general(
        left_side, right_side, (((0,), (0,)), ((), ())), preferred_element_type=F32
    )


def contract_cols(left_side, right_side):
    return lax.dot_general(
        left_side, right_side, (((1,), (1,)), ((), ())), preferred_element_type=F32
    )


FORWARD_ID = 1


def neighbour(index, bit):
    return index + bit - 2 * bit * ((index // bit) % 2)


def greet(partners):
    barrier = pltpu.get_barrier_semaphore()
    for partner in partners:
        pl.semaphore_signal(
            barrier, inc=1, device_id=partner, device_id_type=pl.DeviceIdType.MESH
        )
    pl.semaphore_wait(barrier, len(partners))


def forward_near(shards, inputs, visible, bias_qkv, bias_out, gain, shift_vec, bias_units, head_size):
    size = lax.axis_size("tensor")
    rows, width = inputs.shape
    block = shards[0].shape[0]
    cols = [shard.shape[1] for shard in shards]
    full = [(len(ORDER) * block, size * c) for c in cols]
    units = full[2][1]
    tile = 512
    half = block // 2
    attn = cols[0] // 3

    def body(
        a_in, o_in, u_in, d_in, x_ref, visible_ref, bias_qkv_ref, bias_out_ref, gain_ref, shift_ref,
        bias_units_ref, a_out, o_out, u_out, d_out, qkv_ref, context_ref, hidden_ref, active_out,
        slope_out, a_ref, o_ref, u_ref, low_ref, active_ref, slope_ref, local_sem, own_sem, send_sem,
        recv_sem, tile_sem,
    ):
        data_at, tensor_at = lax.axis_index("dp"), lax.axis_index("tensor")
        shard_refs = (a_in, o_in, u_in, d_in)
        places = (a_ref, o_ref, u_ref, d_out)

        def dp_partner(bit):
            return (neighbour(data_at, bit), tensor_at)

        def z_partner(step):
            return (data_at, (tensor_at + step) % size)

        by_x, by_y, by_core = dp_partner(BIT_X), dp_partner(BIT_Y), dp_partner(BIT_CORE)
        greet([by_x, by_y, by_core] + [z_partner(r) for r in range(1, size)])
        copies = {}

        def send(g, slot, source, target, device):
            copy = pltpu.make_async_remote_copy(
                src_ref=source,
                dst_ref=target,
                send_sem=send_sem.at[g, slot],
                recv_sem=recv_sem.at[g, slot],
                device_id=device,
                device_id_type=pl.DeviceIdType.MESH,
            )
            copies[g, slot] = copy
            copy.start()

        def arrived(g, *slots):
            for slot in slots:
                copies[g, slot].wait_recv()

        def part(g, start, count):
            return places[g].at[start : start + count, :]

        def send_column(g):
            own[g].wait()
            arrived(g, 0, 1, 2)
            send(g, 3, part(g, 0, block), part(g, block, block), by_x)
            send(g, 4, part(g, 0, block), part(g, 2 * block, block), by_y)

        def send_corner(g):
            arrived(g, 3, 4)
            send(g, 5, part(g, block, half), part(g, 3 * block, half), by_y)
            send(g, 6, part(g, 2 * block + half, half), part(g, 3 * block + half, half), by_x)
            for k in range(3):
                send(g, 7 + k, part(g, k * block, block), part(g, (4 + k) * block, block), by_core)

        def send_last(g):
            arrived(g, 5, 6)
            send(g, 10, part(g, 3 * block, block), part(g, 7 * block, block), by_core)

        def finish(g):
            arrived(g, 7, 8, 9, 10)

        saves = []

        def save(g, target):
            copy = pltpu.make_async_copy(places[g], target, local_sem.at[g])
            copy.start()
            saves.append(copy)

        own = []
        for g in range(4):
            copy = pltpu.make_async_copy(
                shard_refs[g], places[g].at[0:block, 0 : cols[g]], own_sem.at[g]
            )
            copy.start()
            own.append(copy)
            for r in range(1, size):
                send(
                    g,
                    r - 1,
                    shard_refs[g],
                    places[g].at[0:block, r * cols[g] : (r + 1) * cols[g]],
                    z_partner(r),
                )

        send_column(0)
        send_column(1)
        send_corner(0)
        send_column(2)
        send_corner(1)
        send_last(0)
        finish(0)
        save(0, a_out)

        def project(r, carry):
            at = pl.multiple_of(r * cols[0], 128)
            total = matmul(x_ref[...], a_ref[:, pl.ds(at, cols[0])])
            qkv_ref[:, pl.ds(at, cols[0])] = (total + bias_qkv_ref[:, pl.ds(at, cols[0])]).astype(BF16)
            return carry

        lax.fori_loop(0, size, project, 0)
        scale = float(head_size) ** (-0.5)

        def attend(r, carry):
            at = pl.multiple_of(r * cols[0], 128)
            to = pl.multiple_of(r * attn, 128)
            seen = visible_ref[...] > 0.0
            for start, lanes, held in pairs_of(attn, head_size):
                queries = qkv_ref[:, pl.ds(at + start, lanes)]
                keys = qkv_ref[:, pl.ds(at + attn + start, lanes)]
                values = qkv_ref[:, pl.ds(at + 2 * attn + start, lanes)]
                total = jnp.zeros((rows, lanes), F32)
                for which in range(held):
                    probs = soft_weights(keep_head(queries, which, head_size), keys, seen, scale)
                    total += keep_head(matmul(probs.astype(BF16), values), which, head_size)
                context_ref[:, pl.ds(to + start, lanes)] = total.astype(BF16)
            return carry

        lax.fori_loop(0, size, attend, 0)
        send_last(1)
        send_corner(2)
        send_column(3)
        finish(1)
        save(1, o_out)

        def output(j, carry):
            at = pl.multiple_of(j * 256, 256)
            total = contract_cols(context_ref[...], o_ref[pl.ds(at, 256), :])
            given = x_ref[:, pl.ds(at, 256)].astype(F32)
            hidden_ref[:, pl.ds(at, 256)] = given + total + bias_out_ref[:, pl.ds(at, 256)]
            return carry

        lax.fori_loop(0, width // 256, output, 0)

        def norm(j, carry):
            at = pl.multiple_of(j * 64, 64)
            normed = norm_forward(hidden_ref[pl.ds(at, 64), :], gain_ref[...], shift_ref[...])[0]
            low_ref[pl.ds(at, 64), :] = normed.astype(BF16)
            return carry

        lax.fori_loop(0, rows // 64, norm, 0)
        send_last(2)
        finish(2)
        save(2, u_out)

        def tile_copies(j, at):
            return (
                pltpu.make_async_copy(
                    active_ref.at[:, pl.ds(at, tile)], active_out.at[:, pl.ds(at, tile)], tile_sem.at[0, j]
                ),
                pltpu.make_async_copy(
                    slope_ref.at[:, pl.ds(at, tile)], slope_out.at[:, pl.ds(at, tile)], tile_sem.at[1, j]
                ),
            )

        def raise_up(j, carry):
            at = pl.multiple_of(j * tile, tile)
            total = matmul(low_ref[...], u_ref[:, pl.ds(at, tile)])
            active, slope = activate(total, bias_units_ref[:, pl.ds(at, tile)])
            active_ref[:, pl.ds(at, tile)] = active.astype(BF16)
            slope_ref[:, pl.ds(at, tile)] = slope
            for copy in tile_copies(j, at):
                copy.start()
            return carry

        lax.fori_loop(0, units // tile, raise_up, 0)
        send_corner(3)
        send_last(3)
        finish(3)

        def settle(j, carry):
            for copy in tile_copies(j, pl.multiple_of(j * tile, tile)):
                copy.wait()
            return carry

        lax.fori_loop(0, units // tile, settle, 0)
        for copy in saves:
            copy.wait()
        for copy in copies.values():
            copy.wait_send()

    anywhere, inside = pl.BlockSpec(memory_space=pl.ANY), pl.BlockSpec(memory_space=pltpu.VMEM)
    sent = sum(2 * block * c * size * 7 for c in cols)
    return pl.pallas_call(
        body,
        out_shape=[jax.ShapeDtypeStruct(shape, BF16) for shape in full]
        + [
            jax.ShapeDtypeStruct((rows, full[0][1]), BF16),
            jax.ShapeDtypeStruct((rows, width), BF16),
            jax.ShapeDtypeStruct((rows, width), F32),
            jax.ShapeDtypeStruct((rows, units), BF16),
            jax.ShapeDtypeStruct((rows, units), F32),
        ],
        in_specs=[anywhere] * 4 + [inside] * 7,
        out_specs=[anywhere] * 4 + [inside] * 3 + [anywhere] * 2,
        scratch_shapes=[pltpu.VMEM(shape, BF16) for shape in full[:3]]
        + [
            pltpu.VMEM((rows, width), BF16),
            pltpu.VMEM((rows, units), BF16),
            pltpu.VMEM((rows, units), F32),
            pltpu.SemaphoreType.DMA((4,)),
            pltpu.SemaphoreType.DMA((4,)),
            pltpu.SemaphoreType.DMA((4, 11)),
            pltpu.SemaphoreType.DMA((4, 11)),
            pltpu.SemaphoreType.DMA((2, units // tile)),
        ],
        compiler_params=pltpu.CompilerParams(
            collective_id=FORWARD_ID, has_side_effects=True, vmem_limit_bytes=60 * 2**20
        ),
        cost_estimate=pl.CostEstimate(
            flops=2 * rows * (full[0][1] + width + units) * width,
            bytes_accessed=2 * sent,
            transcendentals=rows * units,
        ),
        name="forward_near",
    )(*shards, inputs, visible, bias_qkv, bias_out, gain, shift_vec, bias_units)


BACKWARD_ID = 2
TILE = 512


def backward_near(mixed_low, normed_low, inputs, context, grad_second, normal, root, gain, visible,
                  active, slope, qkv, weights, vectors, head_size):
    size = lax.axis_size("tensor")
    rows, width = mixed_low.shape
    block = width // len(ORDER)
    middle = width // 2
    half = block // 2
    full = [weight.shape[1] for weight in weights]
    cols = [c // size for c in full]
    attn = cols[0] // 3
    units = full[2]
    A, O, U, D = range(4)
    vector_rows = (6 * width + 2 * full[1] + units) // 128
    v_query, v_value, v_up = 6 * width // 128, (6 * width + full[1]) // 128, (6 * width + 2 * full[1]) // 128
    scale = float(head_size) ** (-0.5)

    def body(
        mixed_ref, mixed_t, normed_t, input_t, context_ref, second_in, normal_in, root_ref, gain_ref,
        visible_ref, active_in, slope_in, qkv_in, a_in, o_in, u_in, d_in, vectors_ref,
        a_out, o_out, u_out, d_out, grad_out, sums_out,
        w_buf, act_buf, slope_buf, gu_ref, grad_ref, low_ref, low_t, gctx_ref, qkv_buf, send_buf,
        send_o, a_plane, o_plane, u_plane, d_plane, a_corner, o_corner, u_corner, d_corner, a_side,
        o_side, u_side, d_side, a_zin, o_zin, u_zin, d_zin, v_ref, v_in, load_sem, second_sem, core_send,
        core_recv, send_sem, recv_sem, v_send, v_recv,
    ):
        data_at, tensor_at = lax.axis_index("dp"), lax.axis_index("tensor")
        planes = (a_plane, o_plane, u_plane, d_plane)
        corners = (a_corner, o_corner, u_corner, d_corner)
        sides = (a_side, o_side, u_side, d_side)
        zins = (a_zin, o_zin, u_zin, d_zin)
        outs = (a_out, o_out, u_out, d_out)
        sources = (send_buf, send_o, send_buf, send_buf)

        def dp_partner(bit):
            return (neighbour(data_at, bit), tensor_at)

        def z_partner(step):
            return (data_at, (tensor_at + size + step) % size)

        by_x, by_y, by_core = dp_partner(BIT_X), dp_partner(BIT_Y), dp_partner(BIT_CORE)

        def column(j, span=TILE):
            return pl.ds(pl.multiple_of(j * span, 128), span)

        def load(row, source, buffer, j):
            return pltpu.make_async_copy(
                source.at[:, column(j)], buffer.at[j % 2], load_sem.at[row, j % 2]
            )

        def over_tiles(count, loads, step):
            for row, source, buffer in loads:
                load(row, source, buffer, 0).start()

            def one(j, carry):
                @pl.when(j + 1 < count)
                def _():
                    for row, source, buffer in loads:
                        load(row, source, buffer, j + 1).start()

                for row, source, buffer in loads:
                    load(row, source, buffer, j).wait()
                step(j)
                return carry

            lax.fori_loop(0, count, one, 0)

        def remote(source, target, send, receive, device):
            return pltpu.make_async_remote_copy(
                src_ref=source,
                dst_ref=target,
                send_sem=send,
                recv_sem=receive,
                device_id=device,
                device_id_type=pl.DeviceIdType.MESH,
            )

        def core_copy(g, j):
            return remote(
                sources[g].at[:, column(j)],
                planes[g].at[:, column(j)],
                core_send.at[g, j],
                core_recv.at[g, j],
                by_core,
            )

        copies = {}

        def send(g, slot, source, target, device):
            copies[g, slot] = remote(
                source, target, send_sem.at[g, slot], recv_sem.at[g, slot], device
            )
            copies[g, slot].start()

        def arrived(g, *slots):
            for slot in slots:
                copies[g, slot].wait_recv()

        def other_tile(g, left_t, right, j):
            sources[g][:, column(j)] = matmul(left_t[middle:, :], right).astype(BF16)
            core_copy(g, j).start()

        def own_tile(g, left_t, right, j):
            core_copy(g, j).wait_recv()
            total = matmul(left_t[:middle, :], right) + planes[g][:, column(j)].astype(F32)
            planes[g][:, column(j)] = total.astype(BF16)

        def send_corner(g):
            plane = planes[g]
            send(g, 0, plane.at[3 * block : 3 * block + half], corners[g].at[0], by_x)
            send(g, 1, plane.at[3 * block + half :], corners[g].at[1], by_y)

        def add_rows(g, start, more):
            def one(j, carry):
                at = column(j, cols[g])
                total = planes[g][start : start + half, at].astype(F32) + more[:, at].astype(F32)
                planes[g][start : start + half, at] = total.astype(BF16)
                return carry

            lax.fori_loop(0, size, one, 0)

        def send_sides(g):
            arrived(g, 0, 1)
            add_rows(g, 2 * block, corners[g].at[0])
            add_rows(g, block + half, corners[g].at[1])
            send(g, 2, planes[g].at[block : 2 * block], sides[g].at[0], by_x)
            send(g, 3, planes[g].at[2 * block : 3 * block], sides[g].at[1], by_y)

        def send_column(g):
            arrived(g, 2, 3)
            for r in range(size):
                at = slice(r * cols[g], (r + 1) * cols[g])
                total = planes[g][:block, at].astype(F32)
                total += sides[g][0, :, at].astype(F32) + sides[g][1, :, at].astype(F32)
                if r == 0:
                    outs[g][...] = total
                else:
                    planes[g][:block, at] = total.astype(BF16)
                    send(g, 3 + r, planes[g].at[:block, at], zins[g].at[r - 1], z_partner(-r))

        def finish(g):
            arrived(g, *range(4, 3 + size))
            total = outs[g][...]
            for r in range(1, size):
                total += zins[g][r - 1].astype(F32)
            outs[g][...] = total

        def feature_rows(k, vector):
            for place, mask in enumerate(ORDER):
                at = data_at
                for bit in (BIT_CORE, BIT_X, BIT_Y):
                    if mask & bit:
                        at = neighbour(at, bit)
                v_ref[0, pl.ds(k * len(ORDER) + at, 1), :] = vector[:, place * 128 : (place + 1) * 128]

        z_near = tensor_at + 1 - 2 * (tensor_at % 2)
        z_across = tensor_at + 2 - 4 * ((tensor_at // 2) % 2)
        v_partners = (by_core, (data_at, z_near), (data_at, z_across), by_x, by_y)

        def v_copy(k):
            return remote(v_ref.at[k], v_in.at[k], v_send.at[k], v_recv.at[k], v_partners[k])

        def v_add(k):
            v_copy(k).wait_recv()
            v_ref[k + 1] = v_ref[k] + v_in[k]

        grad_load = pltpu.make_async_copy(second_in, grad_ref, second_sem)
        grad_load.start()
        greet([by_x, by_y, by_core] + [z_partner(r) for r in range(1, size)])
        for k in range(3):
            feature_rows((1, 4, 5)[k], vectors_ref[k : k + 1, :])

        def gelu_step(j):
            other_tile(D, mixed_t, act_buf[j % 2], j)
            low = (matmul(mixed_ref[...], w_buf[j % 2]) * slope_buf[j % 2]).astype(BF16)
            gu_ref[:, column(j)] = low
            sums = jnp.sum(low.astype(F32), axis=0, keepdims=True)
            count = TILE // 128
            per = cols[U] // TILE
            first = v_up + ((tensor_at + size - j // per) % size) * (cols[U] // 128) + (j % per) * count
            for k in range(count):
                v_ref[0, pl.ds(first + k, 1), :] = sums[:, k * 128 : (k + 1) * 128]

        over_tiles(
            units // TILE,
            [(0, active_in, act_buf), (1, d_in, w_buf), (2, slope_in, slope_buf)],
            gelu_step,
        )
        normal_loads = [
            pltpu.make_async_copy(normal_in.at[:, column(k)], slope_buf.at[k], load_sem.at[2, k])
            for k in range(2)
        ]
        for copy in normal_loads:
            copy.start()
        over_tiles(
            units // TILE,
            [(0, active_in, act_buf)],
            lambda j: own_tile(D, mixed_t, act_buf[j % 2], j),
        )
        send_corner(D)
        grad_load.wait()

        def up_step(j):
            core_copy(D, j).wait_send()
            tile = gu_ref[:, column(j)]
            other_tile(U, normed_t, tile, j)
            grad_ref[...] += contract_cols(tile, w_buf[j % 2])

        over_tiles(units // TILE, [(1, u_in, w_buf)], up_step)
        send_sides(D)

        def own_up(j, carry):
            own_tile(U, normed_t, gu_ref[:, column(j)], j)
            return carry

        lax.fori_loop(0, units // TILE, own_up, 0)
        send_corner(U)

        for copy in normal_loads:
            copy.wait()
        chunk = 64

        def norm_step(j, sums):
            at = pl.ds(pl.multiple_of(j * chunk, chunk), chunk)
            normal_rows = jnp.concatenate([slope_buf[0, at, :], slope_buf[1, at, :]], axis=1)
            grads = grad_ref[at, :]
            hidden, more_gain, more_shift = norm_backward(
                grads, normal_rows, root_ref[at, :], gain_ref[...]
            )
            grad_ref[at, :] = hidden
            low_ref[at, :] = hidden.astype(BF16)
            more = (jnp.sum(hidden, axis=0), more_gain, more_shift)
            return tuple(a + b[None] for a, b in zip(sums, more))

        zero = jnp.zeros((1, width), F32)
        sums = lax.fori_loop(0, rows // chunk, norm_step, (zero, zero, zero))
        for k in range(3):
            feature_rows((0, 2, 3)[k], sums[k])
        for k in range(width // 128):
            at = slice(k * 128, (k + 1) * 128)
            low_t[at, :] = low_ref[:, at].astype(F32).T.astype(BF16)

        def out_step(j):
            gctx_ref[:, column(j)] = matmul(low_ref[...], w_buf[j % 2]).astype(BF16)
            other_tile(O, low_t, context_ref[:, column(j)], j)

        over_tiles(full[O] // TILE, [(1, o_in, w_buf)], out_step)

        def qkv_load(r):
            return pltpu.make_async_copy(
                qkv_in.at[:, column(r, cols[A])], qkv_buf.at[r % 2], load_sem.at[0, r % 2]
            )

        def attend_step(r, carry):
            @pl.when(r + 1 < size)
            def _():
                qkv_load(r + 1).start()

            qkv_load(r).wait()
            slot = r % 2
            seen = visible_ref[...] > 0.0
            for start, lanes, held in pairs_of(attn, head_size):
                queries = qkv_buf[slot, :, start : start + lanes]
                keys = qkv_buf[slot, :, attn + start : attn + start + lanes]
                values = qkv_buf[slot, :, 2 * attn + start : 2 * attn + start + lanes]
                grads = gctx_ref[:, pl.ds(pl.multiple_of(r * attn + start, 128), lanes)]
                grad_q = jnp.zeros((rows, lanes), F32)
                grad_k = jnp.zeros((rows, lanes), F32)
                grad_v = jnp.zeros((rows, lanes), F32)
                for which in range(held):
                    mine = keep_head(grads, which, head_size)
                    query = keep_head(queries, which, head_size)
                    scores = jnp.where(seen, contract_cols(keys, query) * scale, MASKED)
                    exponent = jnp.exp(scores - jnp.max(scores, axis=0, keepdims=True))
                    probs = exponent * (1.0 / jnp.sum(exponent, axis=0, keepdims=True))
                    grad_v += matmul(probs.astype(BF16), mine)
                    grad_probs = contract_cols(values, mine)
                    inner = jnp.sum(probs * grad_probs, axis=0, keepdims=True)
                    grad_scores = (probs * (grad_probs - inner)).astype(BF16)
                    grad_q += keep_head(contract_rows(grad_scores, keys), which, head_size)
                    grad_k += matmul(grad_scores, query)
                low_q = (grad_q * scale).astype(BF16)
                low_v = grad_v.astype(BF16)
                at = r * cols[A] + start
                gu_ref[:, pl.ds(pl.multiple_of(at, 128), lanes)] = low_q
                gu_ref[:, pl.ds(pl.multiple_of(at + attn, 128), lanes)] = (grad_k * scale).astype(BF16)
                gu_ref[:, pl.ds(pl.multiple_of(at + 2 * attn, 128), lanes)] = low_v
                place = ((tensor_at + size - r) % size) * (attn // 128) + start // 128
                v_ref[0, pl.ds(v_query + place, 1), :] = jnp.sum(
                    low_q.astype(F32), axis=0, keepdims=True
                )
                v_ref[0, pl.ds(v_value + place, 1), :] = jnp.sum(
                    low_v.astype(F32), axis=0, keepdims=True
                )
            return carry

        qkv_load(0).start()
        lax.fori_loop(0, size // 2, attend_step, 0)
        for j in range(full[O] // TILE):
            own_tile(O, low_t, context_ref[:, j * TILE : (j + 1) * TILE], j)
        send_column(D)
        lax.fori_loop(size // 2, size, attend_step, 0)
        v_copy(0).start()
        send_sides(U)

        def qkv_step(j):
            core_copy(U, j).wait_send()
            tile = gu_ref[:, column(j)]
            other_tile(A, input_t, tile, j)
            grad_ref[...] += contract_cols(tile, w_buf[j % 2])

        over_tiles(full[A] // TILE, [(1, a_in, w_buf)], qkv_step)
        for j in range(full[A] // TILE, units // TILE):
            core_copy(U, j).wait_send()
        v_add(0)
        v_copy(1).start()

        def own_qkv(j, carry):
            own_tile(A, input_t, gu_ref[:, column(j)], j)
            return carry

        lax.fori_loop(0, full[A] // TILE, own_qkv, 0)
        send_corner(A)
        send_corner(O)
        v_add(1)
        v_copy(2).start()
        for place, mask in enumerate(ORDER):
            at = data_at
            for bit in (BIT_CORE, BIT_X, BIT_Y):
                if mask & bit:
                    at = neighbour(at, bit)
            grad_out[:, pl.ds(pl.multiple_of(at * block, block), block)] = grad_ref[
                :, place * block : (place + 1) * block
            ].astype(BF16)
        finish(D)
        v_add(2)
        send_column(U)
        send_sides(A)
        send_sides(O)
        v_copy(3).start()
        send_column(A)
        send_column(O)
        v_add(3)
        v_copy(4).start()
        finish(U)
        v_add(4)
        sums_out[...] = v_ref[5]
        finish(A)
        finish(O)
        for j in range(full[A] // TILE):
            core_copy(A, j).wait_send()
        for j in range(full[O] // TILE):
            core_copy(O, j).wait_send()
        for k in range(5):
            v_copy(k).wait_send()
        for copy in copies.values():
            copy.wait_send()

    anywhere, inside = pl.BlockSpec(memory_space=pl.ANY), pl.BlockSpec(memory_space=pltpu.VMEM)
    results = pl.pallas_call(
        body,
        out_shape=[jax.ShapeDtypeStruct((block, c), F32) for c in cols]
        + [
            jax.ShapeDtypeStruct((rows, width), BF16),
            jax.ShapeDtypeStruct((vector_rows, 128), F32),
        ],
        in_specs=[inside] * 5 + [anywhere] * 2 + [inside] * 3 + [anywhere] * 7 + [inside],
        out_specs=[inside] * 6,
        scratch_shapes=[
            pltpu.VMEM((2, width, TILE), BF16),
            pltpu.VMEM((2, rows, TILE), BF16),
            pltpu.VMEM((2, rows, TILE), F32),
            pltpu.VMEM((rows, units), BF16),
            pltpu.VMEM((rows, width), F32),
            pltpu.VMEM((rows, width), BF16),
            pltpu.VMEM((width, rows), BF16),
            pltpu.VMEM((rows, full[1]), BF16),
            pltpu.VMEM((2, rows, cols[0]), BF16),
            pltpu.VMEM((middle, units), BF16),
            pltpu.VMEM((middle, full[1]), BF16),
        ]
        + [pltpu.VMEM((middle, c), BF16) for c in full]
        + [pltpu.VMEM((2, half, c), BF16) for c in full]
        + [pltpu.VMEM((2, block, c), BF16) for c in full]
        + [pltpu.VMEM((size - 1, block, c), BF16) for c in cols]
        + [
            pltpu.VMEM((6, vector_rows, 128), F32),
            pltpu.VMEM((5, vector_rows, 128), F32),
            pltpu.SemaphoreType.DMA((3, 2)),
            pltpu.SemaphoreType.DMA,
            pltpu.SemaphoreType.DMA((4, units // TILE)),
            pltpu.SemaphoreType.DMA((4, units // TILE)),
            pltpu.SemaphoreType.DMA((4, 3 + size)),
            pltpu.SemaphoreType.DMA((4, 3 + size)),
            pltpu.SemaphoreType.DMA((5,)),
            pltpu.SemaphoreType.DMA((5,)),
        ],
        compiler_params=pltpu.CompilerParams(
            collective_id=BACKWARD_ID, has_side_effects=True, vmem_limit_bytes=63 * 2**20
        ),
        cost_estimate=pl.CostEstimate(
            flops=4 * rows * sum(full) * width,
            bytes_accessed=4 * sum(full) * width,
            transcendentals=0,
        ),
        name="backward_near",
    )(
        mixed_low, mixed_low.T, normed_low.T, inputs.T, context, grad_second, normal, root, gain,
        visible, active, slope, qkv, *weights, vectors,
    )
    return results[:4], results[4], results[5]


def gather_far(shard):
    return lax.all_gather(
        lax.all_gather(shard, "tensor", axis=1, tiled=True), "dp", axis=0, tiled=True
    )


def scatter_far(left_side, right_side):
    whole = contract_rows(left_side, right_side).astype(BF16)
    part = lax.psum_scatter(whole, "dp", scatter_dimension=0, tiled=True)
    return lax.psum_scatter(part, "tensor", scatter_dimension=1, tiled=True).astype(F32)


def permute_blocks(array, index, width):
    def body(index_ref, in_ref, out_ref):
        for k in range(array.shape[1] // width):
            start = pl.multiple_of(index_ref[k] * width, width)
            out_ref[:, k * width : (k + 1) * width] = in_ref[:, pl.ds(start, width)]

    return pl.pallas_call(
        body,
        out_shape=jax.ShapeDtypeStruct(array.shape, array.dtype),
        grid_spec=pltpu.PrefetchScalarGridSpec(
            num_scalar_prefetch=1,
            grid=(1,),
            in_specs=[pl.BlockSpec(array.shape, lambda k, index_ref: (0, 0))],
            out_specs=pl.BlockSpec(array.shape, lambda k, index_ref: (0, 0)),
        ),
        cost_estimate=pl.CostEstimate(
            flops=0, bytes_accessed=2 * array.size * array.dtype.itemsize, transcendentals=0
        ),
        name="permute_blocks",
    )(index, array)


def soft_weights(queries, keys, visible, scale):
    scores = contract_cols(queries, keys) * scale
    scores = jnp.where(visible, scores, MASKED)
    exponent = jnp.exp(scores - jnp.max(scores, axis=-1, keepdims=True))
    return exponent * (1.0 / jnp.sum(exponent, axis=-1, keepdims=True))


def pairs_of(width, head_size):
    lanes = max(128, head_size)
    return [(start, lanes, lanes // head_size) for start in range(0, width, lanes)]


def keep_head(array, which, head_size):
    lane = lax.broadcasted_iota(jnp.int32, array.shape, 1)
    return jnp.where(lane // head_size == which, array, jnp.zeros_like(array))


def attend_forward(qkv_q, qkv_kv, length, head_size, groups):
    q_rows = qkv_q.shape[0]
    k_rows = qkv_kv.shape[0]
    block = qkv_q.shape[1] // groups
    width = block // 3
    scale = float(head_size) ** (-0.5)

    def body(length_ref, q_ref, kv_ref, out_ref):
        visible = lax.broadcasted_iota(jnp.int32, (q_rows, k_rows), 1) < length_ref[0]
        for start, lanes, held in pairs_of(width, head_size):
            queries = q_ref[:, start : start + lanes]
            keys = kv_ref[:, width + start : width + start + lanes]
            values = kv_ref[:, 2 * width + start : 2 * width + start + lanes]
            total = jnp.zeros((q_rows, lanes), F32)
            for which in range(held):
                probs = soft_weights(keep_head(queries, which, head_size), keys, visible, scale)
                total += keep_head(matmul(probs.astype(BF16), values), which, head_size)
            out_ref[:, start : start + lanes] = total.astype(BF16)

    return pl.pallas_call(
        body,
        out_shape=jax.ShapeDtypeStruct((q_rows, groups * width), BF16),
        grid_spec=pltpu.PrefetchScalarGridSpec(
            num_scalar_prefetch=1,
            grid=(groups,),
            in_specs=[
                pl.BlockSpec((q_rows, block), lambda g, length_ref: (0, g)),
                pl.BlockSpec((k_rows, block), lambda g, length_ref: (0, g)),
            ],
            out_specs=pl.BlockSpec((q_rows, width), lambda g, length_ref: (0, g)),
        ),
        cost_estimate=pl.CostEstimate(
            flops=4 * q_rows * k_rows * width * groups,
            bytes_accessed=2 * (2 * q_rows + 2 * k_rows) * width * groups,
            transcendentals=q_rows * k_rows * groups * width // head_size,
        ),
        name="attend_forward",
    )(length, qkv_q, qkv_kv)


def attend_backward(qkv_q, qkv_kv, grad_context, length, head_size, groups):
    q_rows = qkv_q.shape[0]
    k_rows = qkv_kv.shape[0]
    block = qkv_q.shape[1] // groups
    width = block // 3
    scale = float(head_size) ** (-0.5)

    def body(length_ref, q_ref, kv_ref, grad_ref, dq_ref, dkv_ref):
        visible = lax.broadcasted_iota(jnp.int32, (q_rows, k_rows), 1) < length_ref[0]
        for start, lanes, held in pairs_of(width, head_size):
            queries = q_ref[:, start : start + lanes]
            keys = kv_ref[:, width + start : width + start + lanes]
            values = kv_ref[:, 2 * width + start : 2 * width + start + lanes]
            grads = grad_ref[:, start : start + lanes]
            grad_q = jnp.zeros((q_rows, lanes), F32)
            grad_k = jnp.zeros((k_rows, lanes), F32)
            grad_v = jnp.zeros((k_rows, lanes), F32)
            for which in range(held):
                mine = keep_head(grads, which, head_size)
                query = keep_head(queries, which, head_size)
                probs = soft_weights(query, keys, visible, scale)
                grad_v += contract_rows(probs.astype(BF16), mine)
                grad_probs = contract_cols(mine, values)
                inner = jnp.sum(probs * grad_probs, axis=-1, keepdims=True)
                grad_scores = (probs * (grad_probs - inner)).astype(BF16)
                grad_q += keep_head(matmul(grad_scores, keys), which, head_size)
                grad_k += contract_rows(grad_scores, query)
            dq_ref[:, start : start + lanes] = (grad_q * scale).astype(BF16)
            dkv_ref[:, start : start + lanes] = (grad_k * scale).astype(BF16)
            dkv_ref[:, width + start : width + start + lanes] = grad_v.astype(BF16)

    return pl.pallas_call(
        body,
        out_shape=(
            jax.ShapeDtypeStruct((q_rows, groups * width), BF16),
            jax.ShapeDtypeStruct((k_rows, groups * 2 * width), BF16),
        ),
        grid_spec=pltpu.PrefetchScalarGridSpec(
            num_scalar_prefetch=1,
            grid=(groups,),
            in_specs=[
                pl.BlockSpec((q_rows, block), lambda g, length_ref: (0, g)),
                pl.BlockSpec((k_rows, block), lambda g, length_ref: (0, g)),
                pl.BlockSpec((q_rows, width), lambda g, length_ref: (0, g)),
            ],
            out_specs=[
                pl.BlockSpec((q_rows, width), lambda g, length_ref: (0, g)),
                pl.BlockSpec((k_rows, 2 * width), lambda g, length_ref: (0, g)),
            ],
        ),
        cost_estimate=pl.CostEstimate(
            flops=10 * q_rows * k_rows * width * groups,
            bytes_accessed=2 * (3 * q_rows + 4 * k_rows) * width * groups,
            transcendentals=q_rows * k_rows * groups * width // head_size,
        ),
        name="attend_backward",
    )(length, qkv_q, qkv_kv, grad_context)


def activate(total, bias):
    upper = total + bias
    cumulative = 0.5 * (1.0 + lax.erf(upper * math.sqrt(0.5)))
    density = jnp.exp(-0.5 * upper * upper) * (1.0 / math.sqrt(2.0 * math.pi))
    return upper * cumulative, cumulative + upper * density


def norm_forward(hidden, gain_vec, shift_vec):
    center = hidden - jnp.mean(hidden, axis=-1, keepdims=True)
    variance = jnp.mean(center * center, axis=-1, keepdims=True)
    inv_root = lax.rsqrt(variance + EPSILON)
    normal = center * inv_root
    return (normal * gain_vec + shift_vec, normal, inv_root)


def norm_backward(grad_in, normal, inv_root, gain_vec):
    grad_normal = grad_in * gain_vec
    grad_gain = jnp.sum(grad_in * normal, axis=0)
    grad_shift = jnp.sum(grad_in, axis=0)
    grad_hidden = inv_root * (
        grad_normal
        - jnp.mean(grad_normal, axis=-1, keepdims=True)
        - normal * jnp.mean(grad_normal * normal, axis=-1, keepdims=True)
    )
    return (grad_hidden, grad_gain, grad_shift)


def layer(
    hidden_in,
    cotangent,
    w_query,
    w_key,
    w_value,
    w_out,
    w_up,
    w_down,
    bias_query,
    bias_value,
    bias_out,
    bias_up,
    bias_down,
    gain_attn,
    shift_attn,
    gain_ffn,
    shift_ffn,
    valid_lengths,
):
    rows, model_width = hidden_in.shape
    n_tensor = lax.axis_size("tensor")
    n_data = lax.axis_size("dp")
    tensor_at = lax.axis_index("tensor")
    data_at = lax.axis_index("dp")
    seq_len = rows * n_tensor // valid_lengths.shape[0]
    spread_over = seq_len // rows
    head_size = model_width // HEADS
    head_cols = w_query.shape[1]
    factor = 1.0 / math.sqrt(rows * n_tensor * n_data)
    near = n_data == len(ORDER) and spread_over == 1
    width = model_width // n_data

    if near:
        order = jnp.array(ORDER, jnp.int32)
        back = jnp.array([ORDER.index(k) for k in range(n_data)], jnp.int32)
        block_at = jnp.bitwise_xor(order, data_at)
        place_of = back[jnp.bitwise_xor(jnp.arange(n_data, dtype=jnp.int32), data_at)]
        column_at = (tensor_at - jnp.arange(n_tensor)) % n_tensor
    else:
        column_at = jnp.arange(n_tensor)

    def arrange(array):
        return permute_blocks(array, block_at, width) if near else array

    def restore(array):
        return permute_blocks(array, place_of, width) if near else array

    def column_vector(vector):
        return vector.reshape(n_tensor, -1)[column_at] if near else vector.reshape(n_tensor, -1)

    vectors = jnp.stack([bias_out, bias_down, gain_attn, shift_attn, gain_ffn, shift_ffn])
    if near:
        vectors = vectors.reshape(-1, n_data, width)[:, block_at].reshape(-1, model_width)
    bias_out, bias_down, gain_attn, shift_attn, gain_ffn, shift_ffn = vectors
    query_bias, value_bias = column_vector(bias_query), column_vector(bias_value)
    bias_qkv = jnp.concatenate(
        [query_bias, jnp.zeros_like(query_bias), value_bias], axis=1
    ).reshape(1, -1)
    bias_units = column_vector(bias_up).reshape(1, -1)
    length = lax.dynamic_slice_in_dim(valid_lengths, tensor_at // spread_over, 1)

    inputs = arrange(hidden_in)
    grad_output = arrange(cotangent).astype(F32)

    w_attend = jnp.concatenate([w_query.astype(BF16), w_key.astype(BF16), w_value.astype(BF16)], axis=1)
    shards = (w_attend, w_out.astype(BF16), w_up.astype(BF16), w_down.astype(BF16))
    if near:
        visible = (jnp.arange(seq_len)[None, :] < length).astype(F32)
        qkv_full, out_full, up_full, down_full, qkv, context, hidden, active, slope = forward_near(
            shards, inputs, visible, bias_qkv, bias_out[None], gain_attn[None], shift_attn[None],
            bias_units, head_size,
        )
        qkv_seq = qkv
    else:
        qkv_full, out_full, up_full, down_full = (gather_far(shard) for shard in shards)
        qkv = (matmul(inputs, qkv_full) + bias_qkv).astype(BF16)
        members = [
            list(range(k, k + spread_over)) for k in range(0, n_tensor, spread_over)
        ]
        qkv_seq = lax.all_gather(qkv, "tensor", axis_index_groups=members, axis=0, tiled=True)
        context = attend_forward(qkv, qkv_seq, length, head_size, n_tensor)
        hidden = inputs.astype(F32) + contract_cols(context, out_full) + bias_out
    normed, normal_attn, root_attn = norm_forward(hidden, gain_attn, shift_attn)
    normed_low = normed.astype(BF16)
    if not near:
        active, slope = activate(matmul(normed_low, up_full), bias_units)
        active = active.astype(BF16)
    mixed = contract_cols(active, down_full)
    result, normal_ffn, root_ffn = norm_forward(normed + mixed + bias_down, gain_ffn, shift_ffn)

    grad_second, grad_gain_ffn, grad_shift_ffn = norm_backward(
        grad_output, normal_ffn, root_ffn, gain_ffn
    )
    grad_bias_down = jnp.sum(grad_second, axis=0)
    mixed_low = grad_second.astype(BF16)
    output = restore(result.astype(BF16))
    if near:
        given = jnp.stack([grad_bias_down, grad_gain_ffn, grad_shift_ffn])
        (grad_qkv_w, grad_out, grad_up, grad_down), grad_input, sums = backward_near(
            mixed_low, normed_low, inputs, context, grad_second, normal_attn, root_attn,
            gain_attn[None], visible.T, active, slope, qkv,
            (qkv_full, out_full, up_full, down_full), given, head_size,
        )
        sums = sums.reshape(-1) * factor
    else:
        grad_down = scatter_far(mixed_low, active)
        grad_upper = (matmul(mixed_low, down_full) * slope).astype(BF16)
        grad_bias_up = jnp.sum(grad_upper, axis=0, dtype=F32)
        grad_up = scatter_far(normed_low, grad_upper)
        grad_normed = grad_second + contract_cols(grad_upper, up_full)
        grad_first, grad_gain_attn, grad_shift_attn = norm_backward(
            grad_normed, normal_attn, root_attn, gain_attn
        )
        grad_bias_out = jnp.sum(grad_first, axis=0)
        attn_low = grad_first.astype(BF16)
        grad_context = matmul(attn_low, out_full).astype(BF16)
        grad_out = scatter_far(attn_low, context)
        grad_q, grad_kv = attend_backward(qkv, qkv_seq, grad_context, length, head_size, n_tensor)
        grad_kv = lax.psum_scatter(
            grad_kv.astype(F32),
            "tensor",
            scatter_dimension=0,
            axis_index_groups=members,
            tiled=True,
        ).astype(BF16)
        grad_qkv = jnp.concatenate(
            [grad_q.reshape(rows, n_tensor, -1), grad_kv.reshape(rows, n_tensor, -1)], axis=2
        ).reshape(rows, -1)
        grad_bias_qkv = jnp.sum(grad_qkv, axis=0, dtype=F32).reshape(n_tensor, 3, head_cols)
        grad_qkv_w = scatter_far(inputs, grad_qkv)
        grad_input = (grad_first + contract_cols(grad_qkv, qkv_full)).astype(BF16)
        sums = jnp.concatenate(
            [
                grad_bias_out,
                grad_bias_down,
                grad_gain_attn,
                grad_shift_attn,
                grad_gain_ffn,
                grad_shift_ffn,
                grad_bias_qkv[:, 0].reshape(-1),
                grad_bias_qkv[:, 2].reshape(-1),
                grad_bias_up,
            ]
        )
        sums = lax.psum(sums, ("dp", "tensor")) * factor
    v_out, v_down, v_gain_attn, v_shift_attn, v_gain_ffn, v_shift_ffn, v_query, v_value = (
        sums[k * model_width : (k + 1) * model_width] for k in range(8)
    )
    v_up = sums[8 * model_width :]
    return (
        output,
        grad_input,
        grad_qkv_w[:, :head_cols] * factor,
        grad_qkv_w[:, head_cols : 2 * head_cols] * factor,
        grad_qkv_w[:, 2 * head_cols :] * factor,
        grad_out * factor,
        grad_up * factor,
        grad_down * factor,
        v_query,
        v_value,
        v_out,
        v_up,
        v_down,
        v_gain_attn,
        v_shift_attn,
        v_gain_ffn,
        v_shift_ffn,
    )


def solution(mesh):
    tokens, matrix, copied = P(("dp", "tensor"), None), P("dp", "tensor"), P()
    return jax.shard_map(
        layer,
        mesh=mesh,
        in_specs=(tokens,) * 2 + (matrix,) * 6 + (copied,) * 9 + (P("dp"),),
        out_specs=(tokens,) * 2 + (matrix,) * 6 + (copied,) * 9,
        check_vma=False,
    )
```

profile of v0, /device:TPU:0, one launch (start us, length us, event | category | flops | bytes accessed | tf_op | source)
XLA Modules:
  0.0 362.2 jit_solution(1767923928483805454)
XLA Ops:
  0.7 1.4 dynamic_slice.3
  2.1 1.2 broadcast_xor_fusion
  3.2 1.2 compare_convert_fusion.visible_ref
  4.5 1.8 gather_fusion
  6.3 0.7 reshape.221
  7.0 0.6 gather_fusion.1
  7.6 0.7 reshape.222
  8.3 0.6 gather_fusion.2
  8.8 0.6 copy.44
  9.5 0.7 reshape.224
  10.2 0.6 gather_fusion.4
  10.7 0.6 copy.45
  11.4 0.8 stack.39
  12.7 0.6 fusion.15
  13.4 0.9 convert_element_type.35
  14.3 0.9 convert_element_type.36
  15.2 0.9 convert_element_type.37
  16.1 0.7 pad_maximum_fusion.a_in
  16.8 0.6 convert_element_type.38.o_in
  17.4 1.4 fusion.9.visible_ref
  18.8 0.7 convert_element_type.39.u_in
  19.6 0.7 convert_element_type.40.d_in
  20.3 3.1 permute_blocks.5
  23.4 3.1 permute_blocks.3.x_ref
  26.5 2.3 copy.40
  28.8 138.1 %forward_near.1 = (bf16[1024,3072]{1,0:T(8,128)(2,1)}, bf16[1024,1024]{1,0:T(8,128)(2,1)}, bf16[1024,4096]{1,0:T(8,128)(2,1)}, bf16[1024,4096]{1,0:T(8,128)(2,1)...) custom-call(bf16[128,768]{1,0:T(8,128)(2,1)} %pad_maximum_fusion.a_i, ...), custom_call_target="tpu_custom_call" | custom-call | flops 8589934592 | bytes 44040192 | tf_op jit(solution)/shard_map/forward_near/pallas_call | solution.py:243
  166.9 1.9 reduce_sum.81
  169.5 0.9 copy.43.root_ref
  170.3 1.8 fusion.8
  172.1 1.3 copy.42.normed_t
  173.5 0.6 copy-done.3
  174.1 8.4 %fusion.16 = (f32[512]{0:T(512)S(1)}, f32[512,1024]{1,0:T(8,128)S(1)}) fusion(f32[1024]{0:T(1024)S(1)} %bitcast.81, bf16[512,4096]{1,0:T(8,128)(2,1)} %get-tuple-element.33.active_in, bf16[1024,4096]{1,0:T(8,128)(2,1)} %get-tuple-element.34.d_in, f32[1024]{0:T(1024)S(1)} %bitcast.70, f32[512,1024]{1,0:T(8,128)S(1)} %copy-done.3, f32[1024]{0:T(1024)S(1)} %bitcast.72), kind=kOutput, calls=%fused_computation.70 | convolution fusion | flops 4297588224 | bytes 16791552 | tf_op jit(solution)/shard_map/dot_general | solution.py:31
  182.9 0.8 copy-done.2
  183.8 1.0 fusion.6
  184.8 1.8 fusion.13
  186.6 0.7 pad_maximum_fusion.1.vectors_ref
  187.3 3.1 permute_blocks.4
  190.6 1.3 copy.41.mixed_t
  191.9 1.1 convert_element_type.44.mixed_ref
  193.1 160.0 %backward_near.1 = (f32[128,768]{1,0:T(8,128)}, f32[128,256]{1,0:T(8,128)}, f32[128,1024]{1,0:T(8,128)}, f32[128,1024]{1,0:T(8,128)}, bf16[512,1024]{1,0:T(8,128)(2,1)}, /*index=5*/f32[96,128]{1,0:T(8,128)}) custom-call(bf16[512,1024]{1,0:T(8,128)(2,1)} %convert_element_type.44.mixed_ref, bf16[1024,512]{1,0:T(8,128)(2,1)} %copy.41.mixed_t, ...), custom_call_target="tpu_custom_call" | custom-call | flops 25769803776 | bytes 50331648 | tf_op jit(solution)/shard_map/backward_near/pallas_call | solution.py:640
  353.0 0.9 broadcast_multiply_fusion.3
  354.0 0.6 slice_bitcast_fusion
  354.6 0.6 slice_bitcast_fusion.1
  355.2 1.6 broadcast_multiply_fusion.2
  356.8 1.8 slice_multiply_fusion
  358.6 1.9 broadcast_multiply_fusion.1
  360.4 0.8 broadcast_multiply_fusion
  361.3 1.0 copy.47
  (33 shorter events, 1.8 us)
Async XLA Ops:
  0.7 18.9 %copy-start.6 = (f32[128,1024]{1,0:T(8,128)S(1)}, f32[128,1024]{1,0:T(8,128)}, u32[]{:S(2)}) copy-start(f32[128,1024]{1,0:T(8,128)} %param.27) | copy-start | bytes 1572868
  0.7 18.1 %copy-start.5 = (f32[128,1024]{1,0:T(8,128)S(1)}, f32[128,1024]{1,0:T(8,128)}, u32[]{:S(2)}) copy-start(f32[128,1024]{1,0:T(8,128)} %param.26) | copy-start | bytes 1572868
  0.7 16.1 %copy-start.8 = (f32[128,256]{1,0:T(8,128)S(1)}, f32[128,256]{1,0:T(8,128)}, u32[]{:S(2)}) copy-start(f32[128,256]{1,0:T(8,128)} %param.25) | copy-start | bytes 393220
  166.9 2.2 copy-start
  172.1 2.0 copy-start.3
  182.5 1.2 copy-start.2
  186.6 5.3 %copy-start.1 = (f32[512,1024]{1,0:T(8,128)}, f32[512,1024]{1,0:T(8,128)S(1)}, u32[]{:S(2)}) copy-start(f32[512,1024]{1,0:T(8,128)S(1)} %get-tuple-element.52.second_in) | copy-start | bytes 6291460
  353.0 7.4 %copy-start.7 = (f32[128,1024]{1,0:T(8,128)S(1)}, f32[128,1024]{1,0:T(8,128)}, u32[]{:S(2)}) copy-start(f32[128,1024]{1,0:T(8,128)} %get-tuple-element.45) | copy-start | bytes 1572868
  353.0 8.2 %copy-start.4 = (bf16[512,1024]{1,0:T(8,128)(2,1)S(1)}, bf16[512,1024]{1,0:T(8,128)(2,1)}, u32[]{:S(2)}) copy-start(bf16[512,1024]{1,0:T(8,128)(2,1)} %get-tuple-element.99) | copy-start | bytes 3145732
where the time goes:
time: 364 us; the launch traced here: 362 us
  Pallas kernels  307 us (84%)
  other arithmetic  25.6 us (7%)
  local copies, waits for them, and re-layouts  20 us (5%)
  matrix products  8.42 us (2%)
    pallas_call x1, Pallas kernels, backward_near(): pl.pallas_call(body, out_shape=[jax.ShapeDtypeStruct((block, c), F32) for...  160 us
    pallas_call x1, Pallas kernels, forward_near(): pl.pallas_call(body, out_shape=[jax.ShapeDtypeStruct(shape, BF16) for sha...  138 us
    pallas_call x3, Pallas kernels, permute_blocks(): pl.pallas_call(body, out_shape=jax.ShapeDtypeStruct(array.shape, array.dt...  9.37 us
    dot_general x1, matrix products, contract_cols(): lax.dot_general(left_side, right_side, (((1,), (1,)), ((), ())), preferre...  8.42 us

commit v1 on v0

--- a/solution.py
+++ b/solution.py
@@ -34,10 +34,19 @@
 
 
 FORWARD_ID = 1
+BACKWARD_ID = 2
+TILE = 512
 
 
 def neighbour(index, bit):
     return index + bit - 2 * bit * ((index // bit) % 2)
+
+
+def block_of(index, mask):
+    for bit in (BIT_CORE, BIT_X, BIT_Y):
+        if mask & bit:
+            index = neighbour(index, bit)
+    return index
 
 
 def greet(partners):
@@ -49,26 +58,29 @@
     pl.semaphore_wait(barrier, len(partners))
 
 
-def forward_near(shards, inputs, visible, bias_qkv, bias_out, gain, shift_vec, bias_units, head_size):
+def forward_near(weights, hidden_in, cotangent, wide, bias_query, bias_value, bias_units, lengths, head_size):
     size = lax.axis_size("tensor")
-    rows, width = inputs.shape
-    block = shards[0].shape[0]
-    cols = [shard.shape[1] for shard in shards]
-    full = [(len(ORDER) * block, size * c) for c in cols]
-    units = full[2][1]
-    tile = 512
+    rows, width = hidden_in.shape
+    block = width // len(ORDER)
+    attn, units_each = weights[0].shape[1], weights[4].shape[1]
+    cols = [3 * attn, attn, units_each, units_each]
+    full = [(width, size * c) for c in cols]
+    units = size * units_each
     half = block // 2
-    attn = cols[0] // 3
+    A, O, U, D = range(4)
+    B_OUT, B_DOWN, G_ATTN, S_ATTN, G_FFN, S_FFN = range(6)
 
     def body(
-        a_in, o_in, u_in, d_in, x_ref, visible_ref, bias_qkv_ref, bias_out_ref, gain_ref, shift_ref,
-        bias_units_ref, a_out, o_out, u_out, d_out, qkv_ref, context_ref, hidden_ref, active_out,
-        slope_out, a_ref, o_ref, u_ref, low_ref, active_ref, slope_ref, local_sem, own_sem, send_sem,
-        recv_sem, tile_sem,
+        q_in, k_in, v_in, o_in, u_in, d_in, hidden_raw, cotangent_ref, bias_out_in, bias_down_in,
+        gain_attn_in, shift_attn_in, gain_ffn_in, shift_ffn_in, bias_q_ref, bias_v_ref, bias_u_ref,
+        lengths_ref,
+        a_out, o_out, u_out, d_out, qkv_ref, context_ref, hidden_ref, active_out, slope_out, output_ref,
+        mixed_ref, mixed_t, normed_t, input_t, second_ref, sums_ref, wide_ref,
+        a_ref, o_ref, u_ref, d_ref, x_ref, low_ref, active_ref, slope_ref, local_sem, send_sem, recv_sem,
+        tile_sem,
     ):
         data_at, tensor_at = lax.axis_index("dp"), lax.axis_index("tensor")
-        shard_refs = (a_in, o_in, u_in, d_in)
-        places = (a_ref, o_ref, u_ref, d_out)
+        places = (a_ref, o_ref, u_ref, d_ref)
 
         def dp_partner(bit):
             return (neighbour(data_at, bit), tensor_at)
@@ -77,7 +89,7 @@
             return (data_at, (tensor_at + step) % size)
 
         by_x, by_y, by_core = dp_partner(BIT_X), dp_partner(BIT_Y), dp_partner(BIT_CORE)
-        greet([by_x, by_y, by_core] + [z_partner(r) for r in range(1, size)])
+        owners = [block_of(data_at, mask) for mask in ORDER]
         copies = {}
 
         def send(g, slot, source, target, device):
@@ -99,8 +111,17 @@
         def part(g, start, count):
             return places[g].at[start : start + count, :]
 
+        def send_z(g):
+            for r in range(1, size):
+                send(
+                    g,
+                    r - 1,
+                    places[g].at[0:block, 0 : cols[g]],
+                    places[g].at[0:block, r * cols[g] : (r + 1) * cols[g]],
+                    z_partner(r),
+                )
+
         def send_column(g):
-            own[g].wait()
             arrived(g, 0, 1, 2)
             send(g, 3, part(g, 0, block), part(g, block, block), by_x)
             send(g, 4, part(g, 0, block), part(g, 2 * block, block), by_y)
@@ -116,9 +137,6 @@
             arrived(g, 5, 6)
             send(g, 10, part(g, 3 * block, block), part(g, 7 * block, block), by_core)
 
-        def finish(g):
-            arrived(g, 7, 8, 9, 10)
-
         saves = []
 
         def save(g, target):
@@ -126,44 +144,66 @@
             copy.start()
             saves.append(copy)
 
-        own = []
-        for g in range(4):
-            copy = pltpu.make_async_copy(
-                shard_refs[g], places[g].at[0:block, 0 : cols[g]], own_sem.at[g]
-            )
-            copy.start()
-            own.append(copy)
-            for r in range(1, size):
-                send(
-                    g,
-                    r - 1,
-                    shard_refs[g],
-                    places[g].at[0:block, r * cols[g] : (r + 1) * cols[g]],
-                    z_partner(r),
-                )
-
-        send_column(0)
-        send_column(1)
-        send_corner(0)
-        send_column(2)
-        send_corner(1)
-        send_last(0)
-        finish(0)
-        save(0, a_out)
+        for k, ref in enumerate((q_in, k_in, v_in)):
+            a_ref[:block, k * attn : (k + 1) * attn] = ref[...].astype(BF16)
+        o_ref[:block, :attn] = o_in[...].astype(BF16)
+        greet([by_x, by_y, by_core] + [z_partner(r) for r in range(1, size)])
+        send_z(A)
+        send_z(O)
+        u_ref[:block, :units_each] = u_in[...].astype(BF16)
+        send_z(U)
+        d_ref[:block, :units_each] = d_in[...].astype(BF16)
+        send_z(D)
+
+        def lanes_of(owner):
+            return pl.ds(pl.multiple_of(owner * block, block), block)
+
+        def transpose_into(target, source):
+            for k in range(width // 128):
+                at = slice(k * 128, (k + 1) * 128)
+                target[at, :] = source[:, at].astype(F32).T.astype(BF16)
+
+        for place, owner in enumerate(owners):
+            at = slice(place * block, (place + 1) * block)
+            x_ref[:, at] = hidden_raw[:, lanes_of(owner)]
+            for k, ref in enumerate(
+                (bias_out_in, bias_down_in, gain_attn_in, shift_attn_in, gain_ffn_in, shift_ffn_in)
+            ):
+                wide_ref[k : k + 1, at] = ref[:, lanes_of(owner)]
+
+        def vector(k):
+            return wide_ref[k : k + 1, :]
+
+        send_column(A)
+        transpose_into(input_t, x_ref)
+        send_column(O)
+        send_corner(A)
+        send_column(U)
+        send_corner(O)
+        send_last(A)
+        arrived(A, 7, 8, 9, 10)
+        save(A, a_out)
+
+        def column_of(r, span):
+            return pl.ds(pl.multiple_of(((tensor_at + size - r) % size) * span, 128), span)
 
         def project(r, carry):
-            at = pl.multiple_of(r * cols[0], 128)
-            total = matmul(x_ref[...], a_ref[:, pl.ds(at, cols[0])])
-            qkv_ref[:, pl.ds(at, cols[0])] = (total + bias_qkv_ref[:, pl.ds(at, cols[0])]).astype(BF16)
+            at = r * cols[A]
+            total = matmul(x_ref[...], a_ref[:, pl.ds(pl.multiple_of(at, 128), cols[A])])
+            biases = (bias_q_ref[:, column_of(r, attn)], 0.0, bias_v_ref[:, column_of(r, attn)])
+            for k, bias in enumerate(biases):
+                piece = total[:, k * attn : (k + 1) * attn] + bias
+                qkv_ref[:, pl.ds(pl.multiple_of(at + k * attn, 128), attn)] = piece.astype(BF16)
             return carry
 
         lax.fori_loop(0, size, project, 0)
         scale = float(head_size) ** (-0.5)
+        length = lengths_ref[tensor_at]
 
         def attend(r, carry):
-            at = pl.multiple_of(r * cols[0], 128)
+            at = pl.multiple_of(r * cols[A], 128)
             to = pl.multiple_of(r * attn, 128)
-            seen = visible_ref[...] > 0.0
+            seen = lax.broadcasted_iota(jnp.int32, (rows, rows), 1) < length
             for start, lanes, held in pairs_of(attn, head_size):
                 queries = qkv_ref[:, pl.ds(at + start, lanes)]
                 keys = qkv_ref[:, pl.ds(at + attn + start, lanes)]
@@ -176,110 +216,161 @@
             return carry
 
         lax.fori_loop(0, size, attend, 0)
-        send_last(1)
-        send_corner(2)
-        send_column(3)
-        finish(1)
-        save(1, o_out)
+        send_last(O)
+        send_corner(U)
+        send_column(D)
+        arrived(O, 7, 8, 9, 10)
+        save(O, o_out)
 
         def output(j, carry):
-            at = pl.multiple_of(j * 256, 256)
-            total = contract_cols(context_ref[...], o_ref[pl.ds(at, 256), :])
-            given = x_ref[:, pl.ds(at, 256)].astype(F32)
-            hidden_ref[:, pl.ds(at, 256)] = given + total + bias_out_ref[:, pl.ds(at, 256)]
+            at = pl.ds(pl.multiple_of(j * 256, 256), 256)
+            total = contract_cols(context_ref[...], o_ref[at, :])
+            hidden_ref[:, at] = x_ref[:, at].astype(F32) + total + wide_ref[B_OUT : B_OUT + 1, at]
             return carry
 
         lax.fori_loop(0, width // 256, output, 0)
+        chunk = 64
 
         def norm(j, carry):
-            at = pl.multiple_of(j * 64, 64)
-            normed = norm_forward(hidden_ref[pl.ds(at, 64), :], gain_ref[...], shift_ref[...])[0]
-            low_ref[pl.ds(at, 64), :] = normed.astype(BF16)
+            at = pl.ds(pl.multiple_of(j * chunk, chunk), chunk)
+            normed = norm_forward(hidden_ref[at, :], vector(G_ATTN), vector(S_ATTN))[0]
+            low_ref[at, :] = normed.astype(BF16)
+            second_ref[at, :] = normed + vector(B_DOWN)
             return carry
 
-        lax.fori_loop(0, rows // 64, norm, 0)
-        send_last(2)
-        finish(2)
-        save(2, u_out)
-
-        def tile_copies(j, at):
-            return (
-                pltpu.make_async_copy(
-                    active_ref.at[:, pl.ds(at, tile)], active_out.at[:, pl.ds(at, tile)], tile_sem.at[0, j]
-                ),
-                pltpu.make_async_copy(
-                    slope_ref.at[:, pl.ds(at, tile)], slope_out.at[:, pl.ds(at, tile)], tile_sem.at[1, j]
-                ),
+        lax.fori_loop(0, rows // chunk, norm, 0)
+        send_last(U)
+        arrived(U, 7, 8, 9, 10)
+        save(U, u_out)
+        per = units_each // TILE
+
+        def tile_at(j):
+            return pl.ds(pl.multiple_of(j * TILE, TILE), TILE)
+
+        def slope_copy(j):
+            return pltpu.make_async_copy(
+                slope_ref.at[j % 2], slope_out.at[:, tile_at(j)], tile_sem.at[1, j % 2]
             )
 
+        def active_copy(j):
+            return pltpu.make_async_copy(
+                active_ref.at[:, tile_at(j)], active_out.at[:, tile_at(j)], tile_sem.at[0, j]
+            )
+
         def raise_up(j, carry):
-            at = pl.multiple_of(j * tile, tile)
-            total = matmul(low_ref[...], u_ref[:, pl.ds(at, tile)])
-            active, slope = activate(total, bias_units_ref[:, pl.ds(at, tile)])
-            active_ref[:, pl.ds(at, tile)] = active.astype(BF16)
-            slope_ref[:, pl.ds(at, tile)] = slope
-            for copy in tile_copies(j, at):
-                copy.start()
+            @pl.when(j >= 2)
+            def _():
+                slope_copy(j - 2).wait()
+
+            total = matmul(low_ref[...], u_ref[:, tile_at(j)])
+            first = ((tensor_at + size - j // per) % size) * units_each + (j % per) * TILE
+            bias = bias_u_ref[:, pl.ds(pl.multiple_of(first, TILE), TILE)]
+            active, slope = activate(total, bias)
+            active_ref[:, tile_at(j)] = active.astype(BF16)
+            slope_ref[j % 2] = slope
+            active_copy(j).start()
+            slope_copy(j).start()
             return carry
 
-        lax.fori_loop(0, units // tile, raise_up, 0)
-        send_corner(3)
-        send_last(3)
-        finish(3)
+        lax.fori_loop(0, units // TILE, raise_up, 0)
+        send_corner(D)
+        transpose_into(normed_t, low_ref)
+
+        def lower(start):
+            at = slice(start, start + 256)
+            second_ref[:, at] += contract_cols(active_ref[...], d_ref[at, :])
+
+        lower(0)
+        arrived(D, 7, 8)
+        lower(4 * block)
+        send_last(D)
+        lower(2 * block)
+        arrived(D, 9, 10)
+        save(D, d_out)
+        lower(6 * block)
+
+        def second(j, sums):
+            at = pl.ds(pl.multiple_of(j * chunk, chunk), chunk)
+            result, normal, root = norm_forward(second_ref[at, :], vector(G_FFN), vector(S_FFN))
+            grads = jnp.concatenate([cotangent_ref[at, lanes_of(owner)] for owner in owners], axis=1)
+            for place, owner in enumerate(owners):
+                output_ref[at, lanes_of(owner)] = result[:, place * block : (place + 1) * block].astype(BF16)
+            hidden, more_gain, more_shift = norm_backward(
+                grads.astype(F32), normal, root, vector(G_FFN)
+            )
+            second_ref[at, :] = hidden
+            mixed_ref[at, :] = hidden.astype(BF16)
+            more = (jnp.sum(hidden, axis=0), more_gain, more_shift)
+            return tuple(a + b[None] for a, b in zip(sums, more))
+
+        zero = jnp.zeros((1, width), F32)
+        sums = lax.fori_loop(0, rows // chunk, second, (zero, zero, zero))
+        for k in range(3):
+            sums_ref[k : k + 1, :] = sums[k]
+        transpose_into(mixed_t, mixed_ref)
 
         def settle(j, carry):
-            for copy in tile_copies(j, pl.multiple_of(j * tile, tile)):
-                copy.wait()
+            active_copy(j).wait()
             return carry
 
-        lax.fori_loop(0, units // tile, settle, 0)
+        lax.fori_loop(0, units // TILE, settle, 0)
+        for j in (units // TILE - 2, units // TILE - 1):
+            slope_copy(j).wait()
         for copy in saves:
             copy.wait()
         for copy in copies.values():
             copy.wait_send()
 
     anywhere, inside = pl.BlockSpec(memory_space=pl.ANY), pl.BlockSpec(memory_space=pltpu.VMEM)
-    sent = sum(2 * block * c * size * 7 for c in cols)
+    tall = jax.ShapeDtypeStruct((rows, width), BF16)
+    turned = jax.ShapeDtypeStruct((width, rows), BF16)
     return pl.pallas_call(
         body,
         out_shape=[jax.ShapeDtypeStruct(shape, BF16) for shape in full]
         + [
-            jax.ShapeDtypeStruct((rows, full[0][1]), BF16),
-            jax.ShapeDtypeStruct((rows, width), BF16),
+            jax.ShapeDtypeStruct((rows, full[A][1]), BF16),
+            tall,
             jax.ShapeDtypeStruct((rows, width), F32),
             jax.ShapeDtypeStruct((rows, units), BF16),
             jax.ShapeDtypeStruct((rows, units), F32),
+            tall,
+            tall,
+            turned,
+            turned,
+            turned,
+            jax.ShapeDtypeStruct((rows, width), F32),
+            jax.ShapeDtypeStruct((3, width), F32),
+            jax.ShapeDtypeStruct((6, width), F32),
         ],
-        in_specs=[anywhere] * 4 + [inside] * 7,
-        out_specs=[anywhere] * 4 + [inside] * 3 + [anywhere] * 2,
-        scratch_shapes=[pltpu.VMEM(shape, BF16) for shape in full[:3]]
+        in_specs=[inside] * 17 + [pl.BlockSpec(memory_space=pltpu.SMEM)],
+        out_specs=[anywhere] * 4 + [inside] * 3 + [anywhere] * 2 + [inside] * 8,
+        scratch_shapes=[pltpu.VMEM(shape, BF16) for shape in full]
         + [
             pltpu.VMEM((rows, width), BF16),
+            pltpu.VMEM((rows, width), BF16),
             pltpu.VMEM((rows, units), BF16),
-            pltpu.VMEM((rows, units), F32),
-            pltpu.SemaphoreType.DMA((4,)),
+            pltpu.VMEM((2, rows, TILE), F32),
             pltpu.SemaphoreType.DMA((4,)),
             pltpu.SemaphoreType.DMA((4, 11)),
             pltpu.SemaphoreType.DMA((4, 11)),
-            pltpu.SemaphoreType.DMA((2, units // tile)),
+            pltpu.SemaphoreType.DMA((2, units // TILE)),
         ],
         compiler_params=pltpu.CompilerParams(
-            collective_id=FORWARD_ID, has_side_effects=True, vmem_limit_bytes=60 * 2**20
+            collective_id=FORWARD_ID, has_side_effects=True, vmem_limit_bytes=63 * 2**20
         ),
         cost_estimate=pl.CostEstimate(
-            flops=2 * rows * (full[0][1] + width + units) * width,
-            bytes_accessed=2 * sent,
+            flops=2 * rows * width * sum(shape[1] for shape in full),
+            bytes_accessed=4 * width * sum(shape[1] for shape in full),
             transcendentals=rows * units,
         ),
         name="forward_near",
-    )(*shards, inputs, visible, bias_qkv, bias_out, gain, shift_vec, bias_units)
-
-
-BACKWARD_ID = 2
-TILE = 512
-
-
-def backward_near(mixed_low, normed_low, inputs, context, grad_second, normal, root, gain, visible,
+    )(
+        *weights, hidden_in, cotangent, *(vector[None] for vector in wide), bias_query[None],
+        bias_value[None], bias_units[None], lengths,
+    )
+
+
+def backward_near(mixed_low, mixed_t, normed_t, input_t, context, grad_second, hidden, wide, lengths,
                   active, slope, qkv, weights, vectors, head_size):
     size = lax.axis_size("tensor")
     rows, width = mixed_low.shape
@@ -296,8 +387,8 @@
     scale = float(head_size) ** (-0.5)
 
     def body(
-        mixed_ref, mixed_t, normed_t, input_t, context_ref, second_in, normal_in, root_ref, gain_ref,
-        visible_ref, active_in, slope_in, qkv_in, a_in, o_in, u_in, d_in, vectors_ref,
+        mixed_ref, mixed_t, normed_t, input_t, context_ref, second_in, hidden_in, wide_ref,
+        lengths_ref, active_in, slope_in, qkv_in, a_in, o_in, u_in, d_in, vectors_ref,
         a_out, o_out, u_out, d_out, grad_out, sums_out,
         w_buf, act_buf, slope_buf, gu_ref, grad_ref, low_ref, low_t, gctx_ref, qkv_buf, send_buf,
         send_o, a_plane, o_plane, u_plane, d_plane, a_corner, o_corner, u_corner, d_corner, a_side,
@@ -427,10 +518,7 @@
 
         def feature_rows(k, vector):
             for place, mask in enumerate(ORDER):
-                at = data_at
-                for bit in (BIT_CORE, BIT_X, BIT_Y):
-                    if mask & bit:
-                        at = neighbour(at, bit)
+                at = block_of(data_at, mask)
                 v_ref[0, pl.ds(k * len(ORDER) + at, 1), :] = vector[:, place * 128 : (place + 1) * 128]
 
         z_near = tensor_at + 1 - 2 * (tensor_at % 2)
@@ -466,11 +554,11 @@
             [(0, active_in, act_buf), (1, d_in, w_buf), (2, slope_in, slope_buf)],
             gelu_step,
         )
-        normal_loads = [
-            pltpu.make_async_copy(normal_in.at[:, column(k)], slope_buf.at[k], load_sem.at[2, k])
+        hidden_loads = [
+            pltpu.make_async_copy(hidden_in.at[:, column(k)], slope_buf.at[k], load_sem.at[2, k])
             for k in range(2)
         ]
-        for copy in normal_loads:
+        for copy in hidden_loads:
             copy.start()
         over_tiles(
             units // TILE,
@@ -496,17 +584,16 @@
         lax.fori_loop(0, units // TILE, own_up, 0)
         send_corner(U)
 
-        for copy in normal_loads:
+        for copy in hidden_loads:
             copy.wait()
         chunk = 64
 
         def norm_step(j, sums):
             at = pl.ds(pl.multiple_of(j * chunk, chunk), chunk)
-            normal_rows = jnp.concatenate([slope_buf[0, at, :], slope_buf[1, at, :]], axis=1)
-            grads = grad_ref[at, :]
-            hidden, more_gain, more_shift = norm_backward(
-                grads, normal_rows, root_ref[at, :], gain_ref[...]
-            )
+            hidden_rows = jnp.concatenate([slope_buf[0, at, :], slope_buf[1, at, :]], axis=1)
+            gain = wide_ref[2:3, :]
+            normal, root = norm_forward(hidden_rows, gain, gain)[1:]
+            hidden, more_gain, more_shift = norm_backward(grad_ref[at, :], normal, root, gain)
             grad_ref[at, :] = hidden
             low_ref[at, :] = hidden.astype(BF16)
             more = (jnp.sum(hidden, axis=0), more_gain, more_shift)
@@ -538,7 +625,7 @@
 
             qkv_load(r).wait()
             slot = r % 2
-            seen = visible_ref[...] > 0.0
+            seen = lax.broadcasted_iota(jnp.int32, (rows, rows), 0) < length
             for start, lanes, held in pairs_of(attn, head_size):
                 queries = qkv_buf[slot, :, start : start + lanes]
                 keys = qkv_buf[slot, :, attn + start : attn + start + lanes]
@@ -574,6 +661,7 @@
                 )
             return carry
 
+        length = lengths_ref[tensor_at]
         qkv_load(0).start()
         lax.fori_loop(0, size // 2, attend_step, 0)
         for j in range(full[O] // TILE):
@@ -605,10 +693,7 @@
         v_add(1)
         v_copy(2).start()
         for place, mask in enumerate(ORDER):
-            at = data_at
-            for bit in (BIT_CORE, BIT_X, BIT_Y):
-                if mask & bit:
-                    at = neighbour(at, bit)
+            at = block_of(data_at, mask)
             grad_out[:, pl.ds(pl.multiple_of(at * block, block), block)] = grad_ref[
                 :, place * block : (place + 1) * block
             ].astype(BF16)
@@ -644,7 +729,11 @@
             jax.ShapeDtypeStruct((rows, width), BF16),
             jax.ShapeDtypeStruct((vector_rows, 128), F32),
         ],
-        in_specs=[inside] * 5 + [anywhere] * 2 + [inside] * 3 + [anywhere] * 7 + [inside],
+        in_specs=[inside] * 5
+        + [anywhere] * 2
+        + [inside, pl.BlockSpec(memory_space=pltpu.SMEM)]
+        + [anywhere] * 7
+        + [inside],
         out_specs=[inside] * 6,
         scratch_shapes=[
             pltpu.VMEM((2, width, TILE), BF16),
@@ -685,8 +774,8 @@
         ),
         name="backward_near",
     )(
-        mixed_low, mixed_low.T, normed_low.T, inputs.T, context, grad_second, normal, root, gain,
-        visible, active, slope, qkv, *weights, vectors,
+        mixed_low, mixed_t, normed_t, input_t, context, grad_second, hidden, wide, lengths, active,
+        slope, qkv, *weights, vectors,
     )
     return results[:4], results[4], results[5]
 
@@ -701,28 +790,6 @@
     whole = contract_rows(left_side, right_side).astype(BF16)
     part = lax.psum_scatter(whole, "dp", scatter_dimension=0, tiled=True)
     return lax.psum_scatter(part, "tensor", scatter_dimension=1, tiled=True).astype(F32)
-
-
-def permute_blocks(array, index, width):
-    def body(index_ref, in_ref, out_ref):
-        for k in range(array.shape[1] // width):
-            start = pl.multiple_of(index_ref[k] * width, width)
-            out_ref[:, k * width : (k + 1) * width] = in_ref[:, pl.ds(start, width)]
-
-    return pl.pallas_call(
-        body,
-        out_shape=jax.ShapeDtypeStruct(array.shape, array.dtype),
-        grid_spec=pltpu.PrefetchScalarGridSpec(
-            num_scalar_prefetch=1,
-            grid=(1,),
-            in_specs=[pl.BlockSpec(array.shape, lambda k, index_ref: (0, 0))],
-            out_specs=pl.BlockSpec(array.shape, lambda k, index_ref: (0, 0)),
-        ),
-        cost_estimate=pl.CostEstimate(
-            flops=0, bytes_accessed=2 * array.size * array.dtype.itemsize, transcendentals=0
-        ),
-        name="permute_blocks",
-    )(index, array)
 
 
 def soft_weights(queries, keys, visible, scale):
@@ -892,88 +959,57 @@
     n_tensor = lax.axis_size("tensor")
     n_data = lax.axis_size("dp")
     tensor_at = lax.axis_index("tensor")
-    data_at = lax.axis_index("dp")
-    seq_len = rows * n_tensor // valid_lengths.shape[0]
-    spread_over = seq_len // rows
+    spread_over = rows * n_tensor // valid_lengths.shape[0] // rows
     head_size = model_width // HEADS
     head_cols = w_query.shape[1]
     factor = 1.0 / math.sqrt(rows * n_tensor * n_data)
-    near = n_data == len(ORDER) and spread_over == 1
-    width = model_width // n_data
-
-    if near:
-        order = jnp.array(ORDER, jnp.int32)
-        back = jnp.array([ORDER.index(k) for k in range(n_data)], jnp.int32)
-        block_at = jnp.bitwise_xor(order, data_at)
-        place_of = back[jnp.bitwise_xor(jnp.arange(n_data, dtype=jnp.int32), data_at)]
-        column_at = (tensor_at - jnp.arange(n_tensor)) % n_tensor
-    else:
-        column_at = jnp.arange(n_tensor)
-
-    def arrange(array):
-        return permute_blocks(array, block_at, width) if near else array
-
-    def restore(array):
-        return permute_blocks(array, place_of, width) if near else array
-
-    def column_vector(vector):
-        return vector.reshape(n_tensor, -1)[column_at] if near else vector.reshape(n_tensor, -1)
-
-    vectors = jnp.stack([bias_out, bias_down, gain_attn, shift_attn, gain_ffn, shift_ffn])
-    if near:
-        vectors = vectors.reshape(-1, n_data, width)[:, block_at].reshape(-1, model_width)
-    bias_out, bias_down, gain_attn, shift_attn, gain_ffn, shift_ffn = vectors
-    query_bias, value_bias = column_vector(bias_query), column_vector(bias_value)
-    bias_qkv = jnp.concatenate(
-        [query_bias, jnp.zeros_like(query_bias), value_bias], axis=1
-    ).reshape(1, -1)
-    bias_units = column_vector(bias_up).reshape(1, -1)
-    length = lax.dynamic_slice_in_dim(valid_lengths, tensor_at // spread_over, 1)
-
-    inputs = arrange(hidden_in)
-    grad_output = arrange(cotangent).astype(F32)
-
-    w_attend = jnp.concatenate([w_query.astype(BF16), w_key.astype(BF16), w_value.astype(BF16)], axis=1)
-    shards = (w_attend, w_out.astype(BF16), w_up.astype(BF16), w_down.astype(BF16))
-    if near:
-        visible = (jnp.arange(seq_len)[None, :] < length).astype(F32)
-        qkv_full, out_full, up_full, down_full, qkv, context, hidden, active, slope = forward_near(
-            shards, inputs, visible, bias_qkv, bias_out[None], gain_attn[None], shift_attn[None],
-            bias_units, head_size,
+    matrices = (w_query, w_key, w_value, w_out, w_up, w_down)
+    wide = (bias_out, bias_down, gain_attn, shift_attn, gain_ffn, shift_ffn)
+
+    if n_data == len(ORDER) and spread_over == 1:
+        (
+            qkv_full, out_full, up_full, down_full, qkv, context, hidden, active, slope, output,
+            mixed_low, mixed_t, normed_t, input_t, grad_second, given, arranged,
+        ) = forward_near(
+            matrices, hidden_in, cotangent, wide, bias_query, bias_value, bias_up, valid_lengths,
+            head_size,
         )
-        qkv_seq = qkv
-    else:
-        qkv_full, out_full, up_full, down_full = (gather_far(shard) for shard in shards)
-        qkv = (matmul(inputs, qkv_full) + bias_qkv).astype(BF16)
-        members = [
-            list(range(k, k + spread_over)) for k in range(0, n_tensor, spread_over)
-        ]
-        qkv_seq = lax.all_gather(qkv, "tensor", axis_index_groups=members, axis=0, tiled=True)
-        context = attend_forward(qkv, qkv_seq, length, head_size, n_tensor)
-        hidden = inputs.astype(F32) + contract_cols(context, out_full) + bias_out
-    normed, normal_attn, root_attn = norm_forward(hidden, gain_attn, shift_attn)
-    normed_low = normed.astype(BF16)
-    if not near:
-        active, slope = activate(matmul(normed_low, up_full), bias_units)
-        active = active.astype(BF16)
-    mixed = contract_cols(active, down_full)
-    result, normal_ffn, root_ffn = norm_forward(normed + mixed + bias_down, gain_ffn, shift_ffn)
-
-    grad_second, grad_gain_ffn, grad_shift_ffn = norm_backward(
-        grad_output, normal_ffn, root_ffn, gain_ffn
-    )
-    grad_bias_down = jnp.sum(grad_second, axis=0)
-    mixed_low = grad_second.astype(BF16)
-    output = restore(result.astype(BF16))
-    if near:
-        given = jnp.stack([grad_bias_down, grad_gain_ffn, grad_shift_ffn])
         (grad_qkv_w, grad_out, grad_up, grad_down), grad_input, sums = backward_near(
-            mixed_low, normed_low, inputs, context, grad_second, normal_attn, root_attn,
-            gain_attn[None], visible.T, active, slope, qkv,
-            (qkv_full, out_full, up_full, down_full), given, head_size,
+            mixed_low, mixed_t, normed_t, input_t, context, grad_second, hidden, arranged,
+            valid_lengths, active, slope, qkv, (qkv_full, out_full, up_full, down_full), given,
+            head_size,
         )
         sums = sums.reshape(-1) * factor
     else:
+
+        def column_part(vector):
+            return vector.reshape(n_tensor, -1)
+
+        query_bias, value_bias = column_part(bias_query), column_part(bias_value)
+        bias_qkv = jnp.concatenate(
+            [query_bias, jnp.zeros_like(query_bias), value_bias], axis=1
+        ).reshape(1, -1)
+        length = lax.dynamic_slice_in_dim(valid_lengths, tensor_at // spread_over, 1)
+        low = [matrix.astype(BF16) for matrix in matrices]
+        shards = [jnp.concatenate(low[:3], axis=1)] + low[3:]
+        qkv_full, out_full, up_full, down_full = (gather_far(shard) for shard in shards)
+        qkv = (matmul(hidden_in, qkv_full) + bias_qkv).astype(BF16)
+        members = [list(range(k, k + spread_over)) for k in range(0, n_tensor, spread_over)]
+        qkv_seq = lax.all_gather(qkv, "tensor", axis_index_groups=members, axis=0, tiled=True)
+        context = attend_forward(qkv, qkv_seq, length, head_size, n_tensor)
+        hidden = hidden_in.astype(F32) + contract_cols(context, out_full) + bias_out
+        normed, normal_attn, root_attn = norm_forward(hidden, gain_attn, shift_attn)
+        normed_low = normed.astype(BF16)
+        active, slope = activate(matmul(normed_low, up_full), bias_up)
+        active = active.astype(BF16)
+        mixed = contract_cols(active, down_full)
+        result, normal_ffn, root_ffn = norm_forward(normed + mixed + bias_down, gain_ffn, shift_ffn)
+        output = result.astype(BF16)
+        grad_second, grad_gain_ffn, grad_shift_ffn = norm_backward(
+            cotangent.astype(F32), normal_ffn, root_ffn, gain_ffn
+        )
+        grad_bias_down = jnp.sum(grad_second, axis=0)
+        mixed_low = grad_second.astype(BF16)
         grad_down = scatter_far(mixed_low, active)
         grad_upper = (matmul(mixed_low, down_full) * slope).astype(BF16)
         grad_bias_up = jnp.sum(grad_upper, axis=0, dtype=F32)
@@ -998,7 +1034,7 @@
             [grad_q.reshape(rows, n_tensor, -1), grad_kv.reshape(rows, n_tensor, -1)], axis=2
         ).reshape(rows, -1)
         grad_bias_qkv = jnp.sum(grad_qkv, axis=0, dtype=F32).reshape(n_tensor, 3, head_cols)
-        grad_qkv_w = scatter_far(inputs, grad_qkv)
+        grad_qkv_w = scatter_far(hidden_in, grad_qkv)
         grad_input = (grad_first + contract_cols(grad_qkv, qkv_full)).astype(BF16)
         sums = jnp.concatenate(
             [

time: 364 us -> 317 us (0.87)
  other arithmetic: 25.6 us -> 5.06 us
  local copies, waits for them, and re-layouts: 20 us -> 4.47 us
  matrix products: 8.42 us -> 0 us
    pallas_call x3 -> x0, Pallas kernels: 9.37 us -> none  [permute_blocks(): pl.pallas_call(body, out_shape=jax.ShapeDtypeStruct(array.shape, array.dt...]
    convert_element_type x9 -> x0, other arithmetic: 8.58 us -> none  [the longest x2 2.61 us: layer(): visible = (jnp.arange(seq_len)[None, :] < length).astype(F32)]
    dot_general x1 -> x0, matrix products: 8.42 us -> none  [contract_cols(): lax.dot_general(left_side, right_side, (((1,), (1,)), ((), ())), preferre...]
    pallas_call x1, Pallas kernels: 138 us -> 146 us  [forward_near(): pl.pallas_call(body, out_shape=[jax.ShapeDtypeStruct(shape, BF16) for sha...]
    reduce_sum x5 -> x0, other arithmetic: 5.44 us -> none  [the longest x1 1.92 us: norm_forward(): center = hidden - jnp.mean(hidden, axis=-1, keepdims=True)]
    gather x5 -> x0, local copies, waits for them, and re-layouts: 4.05 us -> none  [the longest x1 1.81 us: layer(): back[jnp.bitwise_xor(jnp.arange(n_data, dtype=jnp.int32), data_at)]]
where the time goes in v1:
time: 317 us; the launch traced here: 316 us
  Pallas kernels  306 us (97%)
  other arithmetic  5.06 us (2%)
  local copies, waits for them, and re-layouts  4.47 us (1%)
    pallas_call x1, Pallas kernels, backward_near(): pl.pallas_call(body, out_shape=[jax.ShapeDtypeStruct((block, c), F32) for...  160 us
    pallas_call x1, Pallas kernels, forward_near(): pl.pallas_call(body, out_shape=[jax.ShapeDtypeStruct(shape, BF16) for sha...  146 us

profile of v1, /device:TPU:0, one launch (start us, length us, event | category | flops | bytes accessed | tf_op | source)
XLA Modules:
  0.0 316.3 jit_solution(15228346431934112303)
XLA Ops:
  0.7 146.2 %forward_near.1 = (bf16[1024,3072]{1,0:T(8,128)(2,1)}, bf16[1024,1024]{1,0:T(8,128)(2,1)}, bf16[1024,4096]{1,0:T(8,128)(2,1)}, bf16[1024,4096]{1,0:T(8,128)(2,1)...) custom-call(f32[128,256]{1,0:T(8,128)} %q_in.1, ...), custom_call_target="tpu_custom_call" | custom-call | flops 12884901888 | bytes 50331648 | tf_op jit(solution)/shard_map/forward_near/pallas_call | solution.py:327
  146.9 159.9 %backward_near.1 = (f32[128,768]{1,0:T(8,128)}, f32[128,256]{1,0:T(8,128)}, f32[128,1024]{1,0:T(8,128)}, f32[128,1024]{1,0:T(8,128)}, bf16[512,1024]{1,0:T(8,128)(2,1)}, /*index=5*/f32[96,128]{1,0:T(8,128)}) custom-call(bf16[512,1024]{1,0:T(8,128)(2,1)} %get-tuple-element.41.mixed_ref, bf16[1024,512]{1,0:T(8,128)(2,1)} %get-tuple-element.42.mixed_t, ...), custom_call_target="tpu_custom_call" | custom-call | flops 25769803776 | bytes 50331648 | tf_op jit(solution)/shard_map/backward_near/pallas_call | solution.py:725
  306.8 0.0 copy-start
  306.8 0.9 broadcast_multiply_fusion.3
  307.7 0.6 slice_bitcast_fusion
  308.3 0.6 slice_bitcast_fusion.1
  308.9 1.9 slice_multiply_fusion
  310.8 2.3 broadcast_multiply_fusion
  313.1 2.3 copy.37
  315.4 0.0 copy-done
  315.4 1.0 copy.38
Async XLA Ops:
  306.8 8.6 %copy-start = (bf16[512,1024]{1,0:T(8,128)(2,1)S(1)}, bf16[512,1024]{1,0:T(8,128)(2,1)}, u32[]{:S(2)}) copy-start(bf16[512,1024]{1,0:T(8,128)(2,1)} %get-tuple-element.95) | copy-start | bytes 3145732
